TPU v7x, 32 devices: a whole 2x2x4 slice. The times are simulated.
32 devices in a mesh: rows: 8 (over z, y), groups: 4 (over x, core).
Axes of the slice: x: 2, y: 2, z: 4, core: 2. Of those that a mesh axis runs over, the one named last changes fastest.
Arguments:
- basis: bfloat16 [8, 131072, 128], P(None, ('rows', 'groups')), may hold values from -6 to 6
- image: bfloat16 [8, 131072, 128], P(None, ('rows', 'groups')), may hold values from -6 to 6
- selection: int32 [8, 64], replicated, may hold values from 0 to 127, all different within a row
Outputs:
- rotated: bfloat16 [8, 131072, 128], P(None, ('rows', 'groups'))
Inputs may be any that keep to these rules, and one draw needn't show every extreme that they name: Each row of selection names 64 different columns.
All inputs are finite; a program needn't handle non-finite values.
Results may differ from a plain program's by a relative error of at most 0.005.
Values may be sent and summed in bfloat16 or wider, within the bound.
A program may use at most 128 MiB of HBM per device.

v0:
```python
import jax
import jax.numpy as jnp
from jax import lax
from jax.sharding import PartitionSpec as P

ITERS = 3


def small_solve(grams, chosen, total_rows):
    gram_s, cross, gram_f = (grams[0], grams[1], grams[2])
    width = gram_s.shape[0]
    coeffs = (jnp.arange(width, dtype=jnp.int32)[:, None] == chosen[None, :]).astype(jnp.float32)
    factor = jnp.linalg.cholesky(gram_f)
    for step in range(ITERS):
        moved = jnp.dot(cross.T, coeffs, precision=lax.Precision.HIGHEST)
        halfway = lax.linalg.triangular_solve(factor, moved, left_side=True, lower=True)
        solved = lax.linalg.triangular_solve(
            factor, halfway, left_side=True, lower=True, transpose_a=True
        )
        metric = (
            jnp.dot(
                solved.T,
                jnp.dot(gram_s, solved, precision=lax.Precision.HIGHEST),
                precision=lax.Precision.HIGHEST,
            )
            / total_rows
        )
        lower = jnp.linalg.cholesky(metric)
        coeffs = lax.linalg.triangular_solve(
            lower, solved, left_side=False, lower=True, transpose_a=True
        )
    return coeffs


def on_device(basis, image, selection):
    total_rows = basis.shape[1] * lax.axis_size("rows") * lax.axis_size("groups")
    gram_s = jnp.einsum("srk,srl->skl", basis, basis, preferred_element_type=jnp.float32)
    cross = jnp.einsum("srk,srl->skl", basis, image, preferred_element_type=jnp.float32)
    gram_f = jnp.einsum("srk,srl->skl", image, image, preferred_element_type=jnp.float32)
    partial_grams = jnp.stack([gram_s, cross, gram_f], axis=1)
    solver = jax.vmap(lambda grams, chosen: small_solve(grams, chosen, total_rows))
    shares = lax.psum_scatter(partial_grams, "groups", scatter_dimension=0, tiled=True)
    summed = lax.psum(shares, "rows")
    grams = summed
    count = shares.shape[0]
    start = lax.axis_index("groups") * count
    mine = lax.dynamic_slice_in_dim(selection, start, count, 0)
    local_coeffs = solver(grams, mine).astype(jnp.bfloat16)
    narrow = lax.all_gather(local_coeffs, "groups", axis=0, tiled=True)
    first = jnp.einsum("srk,skj->srj", basis, narrow, preferred_element_type=jnp.float32)
    second = jnp.einsum("srk,skj->srj", image, narrow, preferred_element_type=jnp.float32)
    return jnp.concatenate([first, second], axis=2).astype(jnp.bfloat16)


def solution(mesh):
    in_specs = (P(None, ("rows", "groups"), None), P(None, ("rows", "groups"), None), P())
    out_specs = P(None, ("rows", "groups"), None)
    return jax.shard_map(
        on_device, mesh=mesh, in_specs=in_specs, out_specs=out_specs, check_vma=False
    )
```

profile of v0, /device:TPU:0, one launch (start us, length us, event | category | flops | bytes accessed | tf_op | source)
XLA Modules:
  0.0 317.1 jit_solution(13355528183286181943)
XLA Ops:
  6.5 8.5 %convolution_bitcast_fusion.2 = f32[8,1,128,128]{3,2,0,1:T(8,128)S(1)} fusion(bf16[8,4096,128]{2,1,0:T(8,128)(2,1)} %param.10), kind=kOutput, calls=%fused_computation.8 | convolution fusion | flops 1073741824 | bytes 8912896 | tf_op jit(solution)/shard_map/srk,srl->skl/dot_general | solution.py:37
  15.0 5.9 %convolution_bitcast_fusion.1 = f32[8,1,128,128]{3,2,0,1:T(8,128)S(1)} fusion(bf16[8,4096,128]{2,1,0:T(8,128)(2,1)} %param.10, bf16[8,4096,128]{2,1,0:T(8,128)(2,1)S(1)} %copy-done.1), kind=kOutput, calls=%fused_computation.7 | convolution fusion | flops 1073741824 | bytes 17301504 | tf_op jit(solution)/shard_map/srk,srl->skl/dot_general | solution.py:38
  21.0 2.6 convolution_bitcast_fusion
  23.7 1.6 copy.51
  26.9 44.3 %all-reduce.6.cloned.1.call-done = f32[8,3,128,128]{2,3,0,1:T(8,128)} async-done(((f32[8,3,128,128]{2,3,0,1:T(8,128)}), f32[8,3,128,128]{2,3,0,1:T(8,128)}) %all-reduce.6.cloned.1.call-update) | async-done | bytes 1572880
  71.1 1.8 constant_dynamic-slice_fusion
  73.0 73.3 %all-reduce.4.cloned.1.call-done = f32[2,3,128,128]{2,3,0,1:T(8,128)} async-done(((f32[2,3,128,128]{2,3,0,1:T(8,128)}), f32[2,3,128,128]{2,3,0,1:T(8,128)}) %all-reduce.4.cloned.1.call-update) | async-done | bytes 393232 | tf_op jit(solution)/shard_map/psum | solution.py:43
  148.3 23.5 %custom-call.16 = f32[2,128,128]{2,1,0:T(8,128)S(1)} custom-call(f32[2,128,128]{2,1,0:T(8,128)S(1)} %fusion.3), custom_call_target="Cholesky" | custom-call | tf_op jit(solution)/shard_map/vmap(jit(cholesky))/cholesky | solution.py:13
  172.0 19.7 %custom-call.34 = f32[2,1,128,128]{2,3,1,0:T(8,128)S(1)} custom-call(f32[2,1,128,128]{3,2,1,0:T(8,128)S(1)} %select_bitcast_fusion), custom_call_target="InvertDiagBlocksLowerTriangular" | custom-call | tf_op jit(solution)/shard_map/vmap()/triangular_solve/custom-call.3 | solution.py:17
  191.7 1.2 fusion.18
  195.0 11.7 %custom-call.27 = f32[2,64,64]{2,1,0:T(8,128)S(1)} custom-call(f32[2,64,64]{2,1,0:T(8,128)S(1)} %fusion.27), custom_call_target="Cholesky" | custom-call | tf_op jit(solution)/shard_map/vmap(jit(cholesky))/cholesky | solution.py:28
  206.9 9.8 %custom-call.28 = f32[2,1,64,64]{2,3,1,0:T(8,128)S(1)} custom-call(f32[2,1,64,64]{3,2,1,0:T(8,128)S(1)} %select_bitcast_fusion.3), custom_call_target="InvertDiagBlocksLowerTriangular" | custom-call | tf_op jit(solution)/shard_map/vmap()/triangular_solve/custom-call.4 | solution.py:29
  217.1 1.3 fusion.17
  219.0 1.2 fusion.20
  220.5 11.7 %custom-call.31 = f32[2,64,64]{2,1,0:T(8,128)S(1)} custom-call(f32[2,64,64]{2,1,0:T(8,128)S(1)} %fusion.25), custom_call_target="Cholesky" | custom-call | tf_op jit(solution)/shard_map/vmap(jit(cholesky))/cholesky | solution.py:28
  232.4 10.0 %custom-call.32 = f32[2,1,64,64]{2,3,1,0:T(8,128)S(1)} custom-call(f32[2,1,64,64]{3,2,1,0:T(8,128)S(1)} %select_bitcast_fusion.2), custom_call_target="InvertDiagBlocksLowerTriangular" | custom-call | tf_op jit(solution)/shard_map/vmap()/triangular_solve/custom-call.4 | solution.py:29
  242.8 1.3 fusion.16
  246.2 11.7 %custom-call.35 = f32[2,64,64]{2,1,0:T(8,128)S(1)} custom-call(f32[2,64,64]{2,1,0:T(8,128)S(1)} %fusion.23), custom_call_target="Cholesky" | custom-call | tf_op jit(solution)/shard_map/vmap(jit(cholesky))/cholesky | solution.py:28
  258.1 9.8 %custom-call.36 = f32[2,1,64,64]{2,3,1,0:T(8,128)S(1)} custom-call(f32[2,1,64,64]{3,2,1,0:T(8,128)S(1)} %select_bitcast_fusion.1), custom_call_target="InvertDiagBlocksLowerTriangular" | custom-call | tf_op jit(solution)/shard_map/vmap()/triangular_solve/custom-call.4 | solution.py:29
  268.3 5.4 %all_gather.3 = bf16[8,128,64]{1,2,0:T(8,128)(2,1)S(1)} all-gather(bf16[2,128,64]{1,2,0:T(8,128)(2,1)S(1)} %fusion.2), channel_id=1, replica_groups=mesh['rows'=8,'groups'=4] {'groups'}, dimensions={0}, use_global_device_ids=true | all-gather | bytes 163840 | tf_op jit(solution)/shard_map/all_gather | solution.py:49
  273.7 8.4 %fusion.1 = bf16[8,4096,64]{1,2,0:T(8,128)(2,1)} fusion(bf16[8,128,64]{1,2,0:T(8,128)(2,1)S(1)} %all_gather.3, bf16[8,4096,128]{2,1,0:T(8,128)(2,1)} %param.11), kind=kOutput, calls=%fused_computation.4 | convolution fusion | flops 538968064 | bytes 12713984 | tf_op jit(solution)/shard_map/srk,skj->srj/dot_general | solution.py:51
  282.1 8.4 %fusion = bf16[8,4096,64]{1,2,0:T(8,128)(2,1)} fusion(bf16[8,128,64]{1,2,0:T(8,128)(2,1)S(1)} %all_gather.3, bf16[8,4096,128]{2,1,0:T(8,128)(2,1)} %param.10), kind=kOutput, calls=%fused_computation.3 | convolution fusion | flops 538968064 | bytes 12713984 | tf_op jit(solution)/shard_map/srk,skj->srj/dot_general | solution.py:50
  290.5 7.8 %pad_maximum_fusion = bf16[8,4096,128]{1,2,0:T(8,128)(2,1)} fusion(bf16[8,4096,64]{1,2,0:T(8,128)(2,1)} %fusion.1, bf16[8,4096,64]{1,2,0:T(8,128)(2,1)} %fusion), kind=kLoop, calls=%fused_computation | loop fusion | flops 16777216 | bytes 16777216 | tf_op jit(solution)/shard_map/concatenate | solution.py:52
  298.3 11.9 %copy.79 = bf16[8,4096,128]{2,1,0:T(8,128)(2,1)} copy(bf16[8,4096,128]{1,2,0:T(8,128)(2,1)} %pad_maximum_fusion) | data formatting | bytes 16777216 | tf_op jit(solution)/shard_map/concatenate | solution.py:52
  (52 shorter events, 10.0 us)
Async XLA Ops:
  6.5 66.4 %copy-start = (s32[8,64]{1,0:T(8,128)S(1)}, s32[8,64]{1,0:T(8,128)}, u32[]{:S(2)}) copy-start(s32[8,64]{1,0:T(8,128)} %param.12) | copy-start | bytes 6148
  6.5 64.6 %all-reduce.6.cloned.1.call-start = ((), (), s32[]{:S(2)}) async-start(), calls=%async_computation.1 | async-start | bytes 3145728
  6.5 8.5 %copy-start.1 = (bf16[8,4096,128]{2,1,0:T(8,128)(2,1)S(1)}, bf16[8,4096,128]{2,1,0:T(8,128)(2,1)}, u32[]{:S(2)}) copy-start(bf16[8,4096,128]{2,1,0:T(8,128)(2,1)} %param.11) | copy-start | bytes 25165828
  21.0 4.6 %copy-start.2 = (u32[32]{0:T(128)S(1)}, u32[32]{0:T(128)}, u32[]{:S(2)}) copy-start(u32[32]{0:T(128)} %constant.92) | copy-start | bytes 388
  25.4 120.9 %all-reduce.4.cloned.1.call-start = ((), (), s32[]{:S(2)}) async-start(), calls=%async_computation | async-start | bytes 786432 | tf_op jit(solution)/shard_map/psum | solution.py:43
Sparse Core Ops, SparseCore 0:
  25.5 45.6 all-reduce.5
  74.5 71.7 all-reduce.3
where the time goes:
time: 318 us; the launch traced here: 317 us
  other arithmetic  118 us (37%)
  waiting for transfers between devices  118 us (37%)
  matrix products  44.3 us (14%)
  local copies, waits for them, and re-layouts  17.2 us (5%)
  between operations  14.4 us (5%)
  blocking collectives  5.42 us (2%)
    psum x1, waiting for transfers between devices, on_device(): summed = lax.psum(shares, 'rows')  73.3 us
    unnamed x3, waiting for transfers between devices  44.3 us
    another operation x10, other arithmetic, small_solve(): lower = jnp.linalg.cholesky(metric)  35.6 us
    another operation x7, other arithmetic, small_solve(): lax.linalg.triangular_solve(lower, solved, left_side=False, lower=True, t...  30 us
    another operation x4, other arithmetic, small_solve(): factor = jnp.linalg.cholesky(gram_f)  23.6 us
    another operation x3, other arithmetic, small_solve(): lax.linalg.triangular_solve(factor, halfway, left_side=True, lower=True,...  19.8 us
    concatenate x1, local copies, waits for them, and re-layouts, on_device(): return jnp.concatenate([first, second], axis=2).astype(jnp.bfloat16)  11.9 us
    dot_general x1, matrix products, on_device(): jnp.einsum('srk,srl->skl', basis, basis, preferred_element_type=jnp.float32)  8.47 us
  transfers between devices with their start and end apart: 2, of which 2 were waited for; matrix products, arithmetic and copies ran while one was open for 0% of the time, Pallas kernels for 0%

commit v1 on v0

--- a/solution.py
+++ b/solution.py
@@ -40,7 +40,7 @@
     partial_grams = jnp.stack([gram_s, cross, gram_f], axis=1)
     solver = jax.vmap(lambda grams, chosen: small_solve(grams, chosen, total_rows))
     shares = lax.psum_scatter(partial_grams, "groups", scatter_dimension=0, tiled=True)
-    summed = lax.psum(shares, "rows")
+    summed = jnp.sum(lax.all_gather(shares, axis_name="rows"), 0)
     grams = summed
     count = shares.shape[0]
     start = lax.axis_index("groups") * count

time: 318 us -> 299 us (0.940)
  waiting for transfers between devices: 118 us -> 105 us
  matrix products: 44.3 us -> 38.7 us
    psum x1 -> x0, waiting for transfers between devices: 73.3 us -> none  [on_device(): summed = lax.psum(shares, 'rows')]
    all_gather x0 -> x1, waiting for transfers between devices: none -> 60.4 us  [on_device(): summed = jnp.sum(lax.all_gather(shares, axis_name='rows'), 0)]
where the time goes in v1:
time: 299 us; the launch traced here: 298 us
  other arithmetic  120 us (40%)
  waiting for transfers between devices  105 us (35%)
  matrix products  38.7 us (13%)
  local copies, waits for them, and re-layouts  14.7 us (5%)
  between operations  14.4 us (5%)
  blocking collectives  5.42 us (2%)
    all_gather x1, waiting for transfers between devices, on_device(): summed = jnp.sum(lax.all_gather(shares, axis_name='rows'), 0)  60.4 us
    unnamed x3, waiting for transfers between devices  44.3 us
    another operation x10, other arithmetic, small_solve(): lower = jnp.linalg.cholesky(metric)  35.6 us
    another operation x7, other arithmetic, small_solve(): lax.linalg.triangular_solve(lower, solved, left_side=False, lower=True, t...  30 us
    another operation x4, other arithmetic, small_solve(): factor = jnp.linalg.cholesky(gram_f)  23.6 us
    another operation x3, other arithmetic, small_solve(): lax.linalg.triangular_solve(factor, halfway, left_side=True, lower=True,...  19.8 us
    concatenate x1, local copies, waits for them, and re-layouts, on_device(): return jnp.concatenate([first, second], axis=2).astype(jnp.bfloat16)  11.9 us
    dot_general x1, matrix products, on_device(): jnp.einsum('srk,skj->srj', image, narrow, preferred_element_type=jnp.floa...  8.41 us
  transfers between devices with their start and end apart: 2, of which 2 were waited for; matrix products, arithmetic and copies ran while one was open for 0% of the time, Pallas kernels for 0%

profile of v1, /device:TPU:0, one launch (start us, length us, event | category | flops | bytes accessed | tf_op | source)
XLA Modules:
  0.0 298.4 jit_solution(9046712516652795404)
XLA Ops:
  6.5 8.4 %convolution_bitcast_fusion.2 = f32[8,1,128,128]{3,2,0,1:T(8,128)S(1)} fusion(bf16[8,4096,128]{2,1,0:T(8,128)(2,1)} %param.10), kind=kOutput, calls=%fused_computation.8 | convolution fusion | flops 1073741824 | bytes 8912896 | tf_op jit(solution)/shard_map/srk,srl->skl/dot_general | solution.py:37
  15.0 5.9 %convolution_bitcast_fusion.1 = f32[8,1,128,128]{3,2,0,1:T(8,128)S(1)} fusion(bf16[8,4096,128]{2,1,0:T(8,128)(2,1)} %param.10, bf16[8,4096,128]{2,1,0:T(8,128)(2,1)S(1)} %copy-done.1), kind=kOutput, calls=%fused_computation.7 | convolution fusion | flops 1073741824 | bytes 17301504 | tf_op jit(solution)/shard_map/srk,srl->skl/dot_general | solution.py:38
  20.8 2.5 convolution_bitcast_fusion
  23.3 1.2 pad_maximum_fusion.1
  24.8 0.6 dynamic-slice
  26.1 44.3 %all-reduce.3.cloned.1.call-done = f32[8,3,128,128]{3,2,0,1:T(8,128)} async-done(((f32[8,3,128,128]{3,2,0,1:T(8,128)}), f32[8,3,128,128]{3,2,0,1:T(8,128)}) %all-reduce.3.cloned.1.call-update) | async-done | bytes 1572880
  70.4 1.8 constant_dynamic-slice_fusion
  72.3 60.4 %all-gather.3.cloned.1.call-done = f32[16,3,128,128]{3,2,0,1:T(8,128)} async-done(((f32[2,3,128,128]{3,2,0,1:T(8,128)}), f32[16,3,128,128]{3,2,0,1:T(8,128)}) %all-gather.3.cloned.1.call-update) | async-done | bytes 3145744 | tf_op jit(solution)/shard_map/all_gather | solution.py:43
  132.7 2.1 reduce_sum.9
  135.2 23.5 %custom-call.16 = f32[2,128,128]{2,1,0:T(8,128)S(1)} custom-call(f32[2,128,128]{2,1,0:T(8,128)S(1)} %fusion.3), custom_call_target="Cholesky" | custom-call | tf_op jit(solution)/shard_map/vmap(jit(cholesky))/cholesky | solution.py:13
  158.9 19.7 %custom-call.34 = f32[2,1,128,128]{2,3,1,0:T(8,128)S(1)} custom-call(f32[2,1,128,128]{3,2,1,0:T(8,128)S(1)} %select_bitcast_fusion), custom_call_target="InvertDiagBlocksLowerTriangular" | custom-call | tf_op jit(solution)/shard_map/vmap()/triangular_solve/custom-call.3 | solution.py:17
  179.2 0.4 fusion.21
  179.9 11.7 %custom-call.27 = f32[2,64,64]{2,1,0:T(8,128)S(1)} custom-call(f32[2,64,64]{2,1,0:T(8,128)S(1)} %fusion.27), custom_call_target="Cholesky" | custom-call | tf_op jit(solution)/shard_map/vmap(jit(cholesky))/cholesky | solution.py:28
  191.9 9.8 %custom-call.28 = f32[2,1,64,64]{2,3,1,0:T(8,128)S(1)} custom-call(f32[2,1,64,64]{3,2,1,0:T(8,128)S(1)} %select_bitcast_fusion.3), custom_call_target="InvertDiagBlocksLowerTriangular" | custom-call | tf_op jit(solution)/shard_map/vmap()/triangular_solve/custom-call.4 | solution.py:29
  202.9 0.4 fusion.20
  203.6 11.7 %custom-call.31 = f32[2,64,64]{2,1,0:T(8,128)S(1)} custom-call(f32[2,64,64]{2,1,0:T(8,128)S(1)} %fusion.25), custom_call_target="Cholesky" | custom-call | tf_op jit(solution)/shard_map/vmap(jit(cholesky))/cholesky | solution.py:28
  215.6 10.0 %custom-call.32 = f32[2,1,64,64]{2,3,1,0:T(8,128)S(1)} custom-call(f32[2,1,64,64]{3,2,1,0:T(8,128)S(1)} %select_bitcast_fusion.2), custom_call_target="InvertDiagBlocksLowerTriangular" | custom-call | tf_op jit(solution)/shard_map/vmap()/triangular_solve/custom-call.4 | solution.py:29
  227.5 11.7 %custom-call.35 = f32[2,64,64]{2,1,0:T(8,128)S(1)} custom-call(f32[2,64,64]{2,1,0:T(8,128)S(1)} %fusion.23), custom_call_target="Cholesky" | custom-call | tf_op jit(solution)/shard_map/vmap(jit(cholesky))/cholesky | solution.py:28
  239.5 9.8 %custom-call.36 = f32[2,1,64,64]{2,3,1,0:T(8,128)S(1)} custom-call(f32[2,1,64,64]{3,2,1,0:T(8,128)S(1)} %select_bitcast_fusion.1), custom_call_target="InvertDiagBlocksLowerTriangular" | custom-call | tf_op jit(solution)/shard_map/vmap()/triangular_solve/custom-call.4 | solution.py:29
  249.6 5.4 %all_gather.11 = bf16[8,128,64]{1,2,0:T(8,128)(2,1)S(1)} all-gather(bf16[2,128,64]{1,2,0:T(8,128)(2,1)S(1)} %fusion.2), channel_id=1, replica_groups=mesh['rows'=8,'groups'=4] {'groups'}, dimensions={0}, use_global_device_ids=true | all-gather | bytes 163840 | tf_op jit(solution)/shard_map/all_gather | solution.py:49
  255.0 8.4 %fusion.1 = bf16[8,4096,64]{1,2,0:T(8,128)(2,1)} fusion(bf16[8,128,64]{1,2,0:T(8,128)(2,1)S(1)} %all_gather.11, bf16[8,4096,128]{2,1,0:T(8,128)(2,1)} %param.11), kind=kOutput, calls=%fused_computation.4 | convolution fusion | flops 538968064 | bytes 12713984 | tf_op jit(solution)/shard_map/srk,skj->srj/dot_general | solution.py:51
  263.4 8.4 %fusion = bf16[8,4096,64]{1,2,0:T(8,128)(2,1)} fusion(bf16[8,128,64]{1,2,0:T(8,128)(2,1)S(1)} %all_gather.11, bf16[8,4096,128]{2,1,0:T(8,128)(2,1)} %param.10), kind=kOutput, calls=%fused_computation.3 | convolution fusion | flops 538968064 | bytes 12713984 | tf_op jit(solution)/shard_map/srk,skj->srj/dot_general | solution.py:50
  271.8 7.8 %pad_maximum_fusion = bf16[8,4096,128]{1,2,0:T(8,128)(2,1)} fusion(bf16[8,4096,64]{1,2,0:T(8,128)(2,1)} %fusion.1, bf16[8,4096,64]{1,2,0:T(8,128)(2,1)} %fusion), kind=kLoop, calls=%fused_computation | loop fusion | flops 16777216 | bytes 16777216 | tf_op jit(solution)/shard_map/concatenate | solution.py:52
  279.6 11.9 %copy.70 = bf16[8,4096,128]{2,1,0:T(8,128)(2,1)} copy(bf16[8,4096,128]{1,2,0:T(8,128)(2,1)} %pad_maximum_fusion) | data formatting | bytes 16777216 | tf_op jit(solution)/shard_map/concatenate | solution.py:52
  (52 shorter events, 6.2 us)
Async XLA Ops:
  6.5 65.6 %copy-start = (s32[8,64]{1,0:T(8,128)S(1)}, s32[8,64]{1,0:T(8,128)}, u32[]{:S(2)}) copy-start(s32[8,64]{1,0:T(8,128)} %param.12) | copy-start | bytes 6148
  6.5 63.8 %all-reduce.3.cloned.1.call-start = ((), (), s32[]{:S(2)}) async-start(), calls=%async_computation.1 | async-start | bytes 3145728
  6.5 8.4 %copy-start.1 = (bf16[8,4096,128]{2,1,0:T(8,128)(2,1)S(1)}, bf16[8,4096,128]{2,1,0:T(8,128)(2,1)}, u32[]{:S(2)}) copy-start(bf16[8,4096,128]{2,1,0:T(8,128)(2,1)} %param.11) | copy-start | bytes 25165828
  20.8 4.0 %copy-start.2 = (u32[32]{0:T(128)S(1)}, u32[32]{0:T(128)}, u32[]{:S(2)}) copy-start(u32[32]{0:T(128)} %constant.93) | copy-start | bytes 388
  24.6 108.1 %all-gather.3.cloned.1.call-start = ((), (), s32[]{:S(2)}) async-start(), calls=%async_computation | async-start | bytes 3538944 | tf_op jit(solution)/shard_map/all_gather | solution.py:43
Sparse Core Ops, SparseCore 0:
  24.7 45.6 all-reduce.2
  72.6 60.0 all-gather.2
